TPU v7x, 256 devices: a 4x2x16 block of a 4x16x16 slice. The times are simulated.
256 devices in a mesh: groups: 2 (over y), seq: 128 (over z, x, core).
Axes of the slice: x: 4, y: 2, z: 16, core: 2. Of those that a mesh axis runs over, the one named last changes fastest.
The devices are a block of a 4x16x16 slice.
Arguments:
- queries: bfloat16 [65536, 2048], P(('groups', 'seq')), parts along dimension 0, may hold values from -20 to 20
- keys: bfloat16 [65536, 2048], P(('groups', 'seq')), parts along dimension 0, may hold values from -20 to 20
- values: bfloat16 [65536, 2048], P(('groups', 'seq')), parts along dimension 0, may hold values from -6 to 6
- block_counts: int32 [128], P('groups'), parts along dimension 0, may hold values from 2 to 6, as said below
- last_tokens: int32 [256], P('groups'), parts along dimension 0, may hold values from 64 to 128
- pack_order: int32 [256], P('groups'), parts along dimension 0, may hold values from 0 to 127, as said below
- decode_slot: int32 [128], P('groups'), parts along dimension 0, may hold values from 0 to 63, each once
Outputs:
- attended: bfloat16 [65536, 2048], P(('groups', 'seq')), parts along dimension 0
- cache_keys: bfloat16 [256, 256, 16, 128], P(('groups', 'seq')), parts along dimension 0
- cache_values: bfloat16 [256, 256, 16, 128], P(('groups', 'seq')), parts along dimension 0
There are 2 independent parts, one for each index of `groups`. A program takes and returns all parts, laid end to end along the dimension named above; each array names one. Nothing has to cross between parts.
Inputs may be any that keep to these rules, and one draw needn't show every extreme that they name: `block_counts`: they sum to 192; the largest equals 6. `pack_order`: each prompt number appears once. The last 1 positions hold null prompts, and the position before them a conditional prompt of 6 blocks. `decode_slot`: each slot appears once.
All inputs are finite; a program needn't handle non-finite values.
Results may differ from a plain program's by a relative error of at most 0.0034.
Values may be sent and summed in bfloat16 or wider, within the bound.
A program may use at most 64 MiB of HBM per device.

v0:
```python
import jax
import jax.numpy as jnp
from jax import lax
from jax.sharding import PartitionSpec as P

HEADS = 16
HEAD_DIM = 128
BLOCK = 128
MAXB = 6
MASKED_SCORE = -1e30


def shifted(block, axis, distance):
    devices = range(lax.axis_size(axis))
    route = [(i - distance, i) for i in devices if i - distance in devices]
    return lax.ppermute(block, axis, route)


def block_tables(block_counts, last_tokens, pack_order, decode_slot, total_blocks, block):
    pair_count = block_counts.shape[0]
    prompts = 2 * pair_count
    prompt_ids = jnp.arange(prompts, dtype=jnp.int32)
    prompt_sizes = jnp.concatenate([block_counts, jnp.ones((pair_count,), jnp.int32)])
    picked = (pack_order[:, None] == prompt_ids[None, :]).astype(jnp.int32)
    packed_sizes = jnp.sum(picked * prompt_sizes[None, :], axis=1)
    packed_tails = jnp.sum(picked * last_tokens[None, :], axis=1)
    block_ends = jnp.cumsum(packed_sizes)
    starts = block_ends - packed_sizes
    blocks = jnp.arange(total_blocks, dtype=jnp.int32)
    member = (
        (starts[None, :] <= blocks[:, None]) & (blocks[:, None] < block_ends[None, :])
    ).astype(jnp.int32)
    position = jnp.sum(member * prompt_ids[None, :], axis=1)
    prompt = jnp.sum(member * pack_order[None, :], axis=1)
    within = blocks - jnp.sum(member * starts[None, :], axis=1)
    is_last = blocks + 1 == jnp.sum(member * block_ends[None, :], axis=1)
    valid_tokens = jnp.where(is_last, jnp.sum(member * packed_tails[None, :], axis=1), block)
    pair_ids = jnp.arange(pair_count, dtype=jnp.int32)
    earlier = (decode_slot[None, :] < decode_slot[:, None]).astype(jnp.int32)
    slot_start = jnp.sum(earlier * (block_counts + 1)[None, :], axis=1)
    pair_of = prompt % pair_count
    owner = (pair_of[:, None] == pair_ids[None, :]).astype(jnp.int32)
    base_slot = jnp.sum(owner * slot_start[None, :], axis=1)
    own_count = jnp.sum(owner * block_counts[None, :], axis=1)
    destination = base_slot + jnp.where(prompt >= pair_count, own_count, within)
    hits = (destination[None, :] == blocks[:, None]).astype(jnp.int32)
    source = jnp.sum(hits * blocks[None, :], axis=1)
    return (position, valid_tokens, source)


def hand_off(paired, source, devices):
    tokens_here = paired.shape[1]
    blocks_here = tokens_here // BLOCK
    splits = devices // HEADS
    slice_len = BLOCK // splits
    outgoing = paired.reshape(2, blocks_here, splits, slice_len, HEADS, HEAD_DIM)
    outgoing = jnp.transpose(outgoing, (4, 2, 0, 1, 3, 5)).reshape(
        devices, 2, blocks_here, slice_len, HEAD_DIM
    )
    arrived = lax.all_to_all(outgoing, "seq", split_axis=0, concat_axis=2, tiled=True)
    ordered = jnp.take(arrived[0], source, axis=1)
    return (ordered[0][None], ordered[1][None])


def attend(queries, paired, position, valid_tokens, own_index, reach):
    tokens_here, features = queries.shape
    blocks_here = tokens_here // BLOCK
    pieces = [paired]
    for distance in range(1, reach + 1):
        needed = min(blocks_here, MAXB - 1 - (distance - 1) * blocks_here)
        tail_part = paired[:, tokens_here - needed * BLOCK :]
        pieces.insert(0, shifted(tail_part, "seq", distance))
    prior_count = MAXB - 1
    window = jnp.concatenate(pieces, axis=1)
    window_blocks = prior_count + blocks_here
    lead_blocks = reach * blocks_here
    padded_docs = jnp.concatenate([jnp.full((lead_blocks,), -1, jnp.int32), position])
    padded_valid = jnp.concatenate([jnp.zeros((lead_blocks,), jnp.int32), valid_tokens])
    first_block = own_index * blocks_here + lead_blocks - prior_count
    window_docs = lax.dynamic_slice_in_dim(padded_docs, first_block, window_blocks)
    window_valid = lax.dynamic_slice_in_dim(padded_valid, first_block, window_blocks)
    own_first = own_index * blocks_here
    query_docs = lax.dynamic_slice_in_dim(position, own_first, blocks_here)
    query_valid = lax.dynamic_slice_in_dim(valid_tokens, own_first, blocks_here)
    token_ids = jnp.arange(BLOCK, dtype=jnp.int32)
    key_docs = jnp.repeat(window_docs, BLOCK)
    key_limit = jnp.repeat(window_valid, BLOCK)
    key_tokens = jnp.tile(token_ids, window_blocks)
    key_order = jnp.arange(window_blocks * BLOCK, dtype=jnp.int32) - prior_count * BLOCK
    query_order = jnp.arange(tokens_here, dtype=jnp.int32)
    allowed = key_docs[None, :] == jnp.repeat(query_docs, BLOCK)[:, None]
    allowed = (
        allowed & (key_order[None, :] <= query_order[:, None]) & (key_tokens < key_limit)[None, :]
    )
    query_ok = jnp.tile(token_ids, blocks_here) < jnp.repeat(query_valid, BLOCK)
    score_scale = HEAD_DIM ** (-0.5)
    query_heads = jnp.moveaxis(queries.reshape(tokens_here, HEADS, HEAD_DIM), 1, 0)
    key_heads = jnp.moveaxis(window[0].reshape(-1, HEADS, HEAD_DIM), 1, 0)
    value_heads = jnp.moveaxis(window[1].reshape(-1, HEADS, HEAD_DIM), 1, 0)

    def one_head(operands):
        query_part, key_part, value_part = operands
        scores = (
            jnp.einsum("qd,kd->qk", query_part, key_part, preferred_element_type=jnp.float32)
            * score_scale
        )
        scores = jnp.where(allowed, scores, MASKED_SCORE)
        peak = jnp.max(scores, axis=1, keepdims=True)
        weights = jnp.exp(scores - peak)
        totals = jnp.sum(weights, axis=1, keepdims=True)
        mixed = jnp.dot(
            weights.astype(jnp.bfloat16), value_part, preferred_element_type=jnp.float32
        )
        return mixed / totals

    head_outputs = lax.map(one_head, (query_heads, key_heads, value_heads))
    merged = jnp.moveaxis(head_outputs, 0, 1).reshape(tokens_here, features)
    return jnp.where(query_ok[:, None], merged, 0.0).astype(jnp.bfloat16)


def local(queries, keys, values, block_counts, last_tokens, pack_order, decode_slot):
    devices = lax.axis_size("seq")
    own_index = lax.axis_index("seq")
    tokens_here = queries.shape[0]
    blocks_here = tokens_here // BLOCK
    reach = (MAXB + blocks_here - 2) // blocks_here
    position, valid_tokens, source = block_tables(
        block_counts, last_tokens, pack_order, decode_slot, blocks_here * devices, BLOCK
    )
    paired = jnp.stack([keys, values])
    attended = attend(queries, paired, position, valid_tokens, own_index, reach)
    cache_keys, cache_values = hand_off(paired, source, devices)
    return (attended, cache_keys, cache_values)


def solution(mesh):
    placed = (
        P(("groups", "seq"), None),
        P(("groups", "seq"), None),
        P(("groups", "seq"), None),
        P("groups"),
        P("groups"),
        P("groups"),
        P("groups"),
    )
    return jax.shard_map(
        local,
        mesh=mesh,
        in_specs=placed,
        out_specs=(
            P(("groups", "seq"), None),
            P(("groups", "seq"), None, None, None),
            P(("groups", "seq"), None, None, None),
        ),
        check_vma=False,
    )
```

profile of v0, /device:TPU:33, one launch (start us, length us, event | category | flops | bytes accessed | tf_op | source)
XLA Modules:
  0.0 243.1 jit_solution(12251069177310898664)
XLA Ops:
  0.6 1.6 copy.37
  2.8 1.5 pad_maximum_fusion
  4.3 5.6 %collective-permute-start.1 = (bf16[2,256,2048]{1,2,0:T(8,128)(2,1)}, bf16[2,256,2048]{1,2,0:T(8,128)(2,1)}, u32[]{:S(2)}, u32[]{:S(2)}) collective-permute-start(bf16[2,256,2048]{1,2,0:T(8,128)(2,1)} %pad_maximum_fusion), channel_id=1, source_target_pairs={{0,2},{1,3},{2,4},{3,5},{4,6},{5,7},{6,8},{7,9},{8,10},{9,11},{10,... | collective-permute-start | bytes 6291464 | tf_op jit(solution)/shard_map/ppermute | solution.py:16
  9.9 2.7 %collective-permute-start.2 = (bf16[2,256,2048]{1,2,0:T(8,128)(2,1)}, bf16[2,256,2048]{1,2,0:T(8,128)(2,1)}, u32[]{:S(2)}, u32[]{:S(2)}) collective-permute-start(bf16[2,256,2048]{1,2,0:T(8,128)(2,1)} %pad_maximum_fusion), channel_id=1, source_target_pairs={{0,1},{1,2},{2,3},{3,4},{4,5},{5,6},{6,7},{7,8},{8,9},{9,10},{10,1... | collective-permute-start | bytes 6291464 | tf_op jit(solution)/shard_map/ppermute | solution.py:16
  13.7 4.3 %collective-permute-start = (bf16[2,128,2048]{1,2,0:T(8,128)(2,1)}, bf16[2,128,2048]{1,2,0:T(8,128)(2,1)}, u32[]{:S(2)}, u32[]{:S(2)}) collective-permute-start(bf16[2,128,2048]{1,2,0:T(8,128)(2,1)} %fusion.20), channel_id=1, source_target_pairs={{0,3},{1,4},{2,5},{3,6},{4,7},{5,8},{6,9},{7,10},{8,11},{9,12},{10... | collective-permute-start | bytes 3145736 | tf_op jit(solution)/shard_map/ppermute | solution.py:16
  18.7 1.9 copy.43
  20.6 28.4 %all-to-all-start = ((bf16[128,2,2,16,128]{4,3,2,1,0:T(8,128)(2,1)}), bf16[128,2,2,16,128]{4,3,2,1,0:T(8,128)(2,1)}, u32[]{:S(2)}, u32[]{:S(2)}) async-start(bf16[128,2,2,16,128]{4,3,2,1,0:T(8,128)(2,1)} %bitcast.84), calls=%async_computation | async-start | bytes 4194304 | tf_op jit(solution)/shard_map/all_to_all | solution.py:60
  50.7 2.3 copy.36
  53.2 62.3 %collective-permute-done = bf16[2,128,2048]{1,2,0:T(8,128)(2,1)} collective-permute-done((bf16[2,128,2048]{1,2,0:T(8,128)(2,1)}, bf16[2,128,2048]{1,2,0:T(8,128)(2,1)}, u32[]{:S(2)}, u32[]{:S(2)}) %collective-permute-start) | collective-permute-done | bytes 1048608 | tf_op jit(solution)/shard_map/ppermute | solution.py:16
  115.5 3.5 %maximum_maximum_fusion = bf16[2,896,2048]{1,2,0:T(8,128)(2,1)S(1)} fusion(bf16[1,256,2048]{1,2,0:T(8,128)(2,1)S(1)} %bitcast.82, bf16[1,256,2048]{1,2,0:T(8,128)(2,1)S(1)} %bitcast.79, bf16[2,256,2048]{1,2,0:T(8,128)(2,1)} %collective-permute-done.2, bf16[2,256,2048]{1,2,0:T(8,128)(2,1)} %collective-permute-done.1, ...), kind=kLoop, calls=%fused_computation.22 | loop fusion | flops 36700160 | bytes 14680064 | tf_op jit(solution)/shard_map/concatenate | solution.py:74
  119.0 3.6 %fusion.26 = (bf16[1,896,2048]{1,2,0:T(8,128)(2,1)}, bf16[1,896,2048]{1,2,0:T(8,128)(2,1)}) fusion(bf16[2,896,2048]{1,2,0:T(8,128)(2,1)S(1)} %maximum_maximum_fusion), kind=kLoop, calls=%fused_computation.71 | loop fusion | bytes 14680064 | tf_op jit(solution)/shard_map/slice | solution.py:99
  122.6 50.8 %while.11 = (s32[]{:T(128)}, bf16[16,256,128]{2,1,0:T(8,128)(2,1)S(1)}, bf16[16,256,128]{1,2,0:T(8,128)(2,1)}, bf16[16,896,128]{1,2,0:T(8,128)(2,1)}, bf16[16,89...) while((s32[]{:T(128)}, ...), condition=%wide.region_9.10_spmd.clone, body=%wide.region_6.0_spmd.clone.sunk | while | flops 119995904 | bytes 3424229 | solution.py:116
  122.6 1.5 fusion.35
  124.4 1.3 fusion.37
  125.7 1.5 fusion.35
  127.6 1.3 fusion.37
  128.9 1.5 fusion.35
  130.8 1.3 fusion.37
  132.1 1.5 fusion.35
  133.9 1.3 fusion.37
  135.3 1.5 fusion.35
  137.1 1.3 fusion.37
  138.5 1.5 fusion.35
  140.3 1.3 fusion.37
  141.6 1.5 fusion.35
  143.5 1.3 fusion.37
  144.8 1.5 fusion.35
  146.6 1.3 fusion.37
  148.0 1.5 fusion.35
  149.8 1.3 fusion.37
  151.2 1.5 fusion.35
  153.0 1.3 fusion.37
  154.3 1.5 fusion.35
  156.2 1.3 fusion.37
  157.5 1.5 fusion.35
  159.3 1.3 fusion.37
  160.7 1.5 fusion.35
  162.5 1.3 fusion.37
  163.9 1.5 fusion.35
  165.7 1.3 fusion.37
  167.0 1.5 fusion.35
  168.9 1.3 fusion.37
  170.2 1.5 fusion.35
  172.0 1.3 fusion.37
  174.6 59.9 %all-to-all-done = bf16[128,2,2,16,128]{4,3,2,1,0:T(8,128)(2,1)} async-done(((bf16[128,2,2,16,128]{4,3,2,1,0:T(8,128)(2,1)}), bf16[128,2,2,16,128]{4,3,2,1,0:T(8,128)(2,1)}, u32[]{:S(2)}, u32[]{:S(2)}) %all-to-all-start) | async-done | bytes 2097184 | tf_op jit(solution)/shard_map/all_to_all | solution.py:60
  234.5 3.3 %copy.44 = bf16[1,2,128,2,16,128]{5,4,3,2,1,0:T(8,128)(2,1)} copy(bf16[1,2,128,2,16,128]{5,4,3,1,2,0:T(8,128)(2,1)} %bitcast.17) | data formatting | bytes 4194304 | tf_op jit(solution)/shard_map/all_to_all | solution.py:60
  237.8 2.7 %gather_fusion = bf16[256,2,16,128]{3,2,1,0:T(8,128)(2,1)S(1)} fusion(bf16[2,256,16,128]{3,2,1,0:T(8,128)(2,1)} %bitcast.83, s32[1024]{0:T(1024)S(1)} %pad_clamp_fusion), kind=kCustom, calls=%fused_computation | custom fusion | bytes 4195328 | tf_op jit(solution)/shard_map/jit(_take)/gather | solution.py:61
  241.4 1.7 slice_bitcast_fusion
  (63 shorter events, 11.1 us)
Async XLA Ops:
  0.6 1.6 copy-start.1
  4.3 13.7 %copy-start = (bf16[256,2048]{1,0:T(8,128)(2,1)S(1)}, bf16[256,2048]{1,0:T(8,128)(2,1)}, u32[]{:S(2)}) copy-start(bf16[256,2048]{1,0:T(8,128)(2,1)} %param.10) | copy-start | bytes 3145732
  4.3 111.2 %collective-permute-start.1 = (bf16[2,256,2048]{1,2,0:T(8,128)(2,1)}, bf16[2,256,2048]{1,2,0:T(8,128)(2,1)}, u32[]{:S(2)}, u32[]{:S(2)}) collective-permute-start(bf16[2,256,2048]{1,2,0:T(8,128)(2,1)} %pad_maximum_fusion), channel_id=1, source_target_pairs={{0,2},{1,3},{2,4},{3,5},{4,6},{5,7},{6,8},{7,9},{8,10},{9,11},{10,... | collective-permute-start | bytes 6291464 | tf_op jit(solution)/shard_map/ppermute | solution.py:16
  9.9 105.7 %collective-permute-start.2 = (bf16[2,256,2048]{1,2,0:T(8,128)(2,1)}, bf16[2,256,2048]{1,2,0:T(8,128)(2,1)}, u32[]{:S(2)}, u32[]{:S(2)}) collective-permute-start(bf16[2,256,2048]{1,2,0:T(8,128)(2,1)} %pad_maximum_fusion), channel_id=1, source_target_pairs={{0,1},{1,2},{2,3},{3,4},{4,5},{5,6},{6,7},{7,8},{8,9},{9,10},{10,1... | collective-permute-start | bytes 6291464 | tf_op jit(solution)/shard_map/ppermute | solution.py:16
  13.7 101.8 %collective-permute-start = (bf16[2,128,2048]{1,2,0:T(8,128)(2,1)}, bf16[2,128,2048]{1,2,0:T(8,128)(2,1)}, u32[]{:S(2)}, u32[]{:S(2)}) collective-permute-start(bf16[2,128,2048]{1,2,0:T(8,128)(2,1)} %fusion.20), channel_id=1, source_target_pairs={{0,3},{1,4},{2,5},{3,6},{4,7},{5,8},{6,9},{7,10},{8,11},{9,12},{10... | collective-permute-start | bytes 3145736 | tf_op jit(solution)/shard_map/ppermute | solution.py:16
  20.6 28.4 %copy-start.5 = (s32[64]{0:T(128)S(1)}, s32[64]{0:T(128)}, u32[]{:S(2)}) copy-start(s32[64]{0:T(128)} %param.12) | copy-start | bytes 772
  20.6 28.4 %copy-start.2 = (s32[128]{0:T(128)S(1)}, s32[128]{0:T(128)}, u32[]{:S(2)}) copy-start(s32[128]{0:T(128)} %param.14) | copy-start | bytes 1540
  20.6 28.4 %copy-start.4 = (s32[128]{0:T(128)S(1)}, s32[128]{0:T(128)}, u32[]{:S(2)}) copy-start(s32[128]{0:T(128)} %param.13) | copy-start | bytes 1540
  20.6 29.4 %copy-start.3 = (s32[64]{0:T(128)S(1)}, s32[64]{0:T(128)}, u32[]{:S(2)}) copy-start(s32[64]{0:T(128)} %param.15) | copy-start | bytes 772
  20.6 213.9 %all-to-all-start = ((bf16[128,2,2,16,128]{4,3,2,1,0:T(8,128)(2,1)}), bf16[128,2,2,16,128]{4,3,2,1,0:T(8,128)(2,1)}, u32[]{:S(2)}, u32[]{:S(2)}) async-start(bf16[128,2,2,16,128]{4,3,2,1,0:T(8,128)(2,1)} %bitcast.84), calls=%async_computation | async-start | bytes 4194304 | tf_op jit(solution)/shard_map/all_to_all | solution.py:60
where the time goes:
time: 244 us; the launch traced here: 243 us
  waiting for transfers between devices  122 us (50%)
  matrix products  45.6 us (19%)
  starting transfers between devices  41 us (17%)
  local copies, waits for them, and re-layouts  18.5 us (8%)
  other arithmetic  14.6 us (6%)
    ppermute x3, waiting for transfers between devices, shifted(): return lax.ppermute(block, axis, route)  62.3 us
    all_to_all x1, waiting for transfers between devices, hand_off(): lax.all_to_all(outgoing, 'seq', split_axis=0, concat_axis=2, tiled=True)  59.9 us
    all_to_all x1, starting transfers between devices, hand_off(): lax.all_to_all(outgoing, 'seq', split_axis=0, concat_axis=2, tiled=True)  28.4 us
    dot_general x16, matrix products, one_head(): jnp.einsum('qd,kd->qk', query_part, key_part, preferred_element_type=jnp....  24.4 us
    dot_general x16, matrix products, one_head(): jnp.dot(weights.astype(jnp.bfloat16), value_part, preferred_element_type=...  21.2 us
    ppermute x3, starting transfers between devices, shifted(): return lax.ppermute(block, axis, route)  12.6 us
    unnamed x18, local copies, waits for them, and re-layouts  6.51 us
  transfers between devices with their start and end apart: 4, of which 2 were waited for; matrix products, arithmetic and copies ran while one was open for 27% of the time, Pallas kernels for 0%

commit v1 on v0

--- a/solution.py
+++ b/solution.py
@@ -57,7 +57,9 @@
     outgoing = jnp.transpose(outgoing, (4, 2, 0, 1, 3, 5)).reshape(
         devices, 2, blocks_here, slice_len, HEAD_DIM
     )
-    arrived = lax.all_to_all(outgoing, "seq", split_axis=0, concat_axis=2, tiled=True)
+    arrived = jnp.concatenate(
+        lax.all_to_all(jnp.stack(jnp.split(outgoing, lax.axis_size("seq"), 0), 0), "seq", 0, 0), 2
+    )
     ordered = jnp.take(arrived[0], source, axis=1)
     return (ordered[0][None], ordered[1][None])
 

time: 244 us -> 233 us (0.955)
  waiting for transfers between devices: 122 us -> 35.5 us
  local copies, waits for them, and re-layouts: 18.5 us -> 94 us
    unnamed x18 -> x145, local copies, waits for them, and re-layouts: 6.51 us -> 82.7 us
    ppermute x3, waiting for transfers between devices: 62.3 us -> 0.01 us  [shifted(): return lax.ppermute(block, axis, route)]
    all_to_all x1, waiting for transfers between devices: 59.9 us -> 35.5 us  [hand_off(): lax.all_to_all(jnp.stack(jnp.split(outgoing, lax.axis_size('seq'), 0), 0)...]
    all_to_all x1 -> x0, local copies, waits for them, and re-layouts: 3.32 us -> none  [hand_off(): lax.all_to_all(outgoing, 'seq', split_axis=0, concat_axis=2, tiled=True)]
    reshape x0 -> x1, local copies, waits for them, and re-layouts: none -> 3.32 us  [hand_off(): jnp.concatenate(lax.all_to_all(jnp.stack(jnp.split(outgoing, lax.axis_siz...]
  transfers between devices with their start and end apart: 4 -> 4, of which waited for: 2 -> 1; matrix products, arithmetic and copies ran while one was open for 27% -> 61% of each run, Pallas kernels for 0% -> 0%
where the time goes in v1:
time: 233 us; the launch traced here: 232 us
  local copies, waits for them, and re-layouts  94 us (40%)
  matrix products  45.7 us (20%)
  starting transfers between devices  40.7 us (17%)
  waiting for transfers between devices  35.5 us (15%)
  other arithmetic  14.8 us (6%)
    unnamed x145, local copies, waits for them, and re-layouts  82.7 us
    all_to_all x1, waiting for transfers between devices, hand_off(): lax.all_to_all(jnp.stack(jnp.split(outgoing, lax.axis_size('seq'), 0), 0)...  35.5 us
    all_to_all x1, starting transfers between devices, hand_off(): lax.all_to_all(jnp.stack(jnp.split(outgoing, lax.axis_size('seq'), 0), 0)...  28.1 us
    dot_general x16, matrix products, one_head(): jnp.einsum('qd,kd->qk', query_part, key_part, preferred_element_type=jnp....  24.4 us
    dot_general x16, matrix products, one_head(): jnp.dot(weights.astype(jnp.bfloat16), value_part, preferred_element_type=...  21.3 us
    ppermute x3, starting transfers between devices, shifted(): return lax.ppermute(block, axis, route)  12.6 us
    reduce_sum x16, other arithmetic, one_head(): totals = jnp.sum(weights, axis=1, keepdims=True)  4.99 us
  transfers between devices with their start and end apart: 4, of which 1 were waited for; matrix products, arithmetic and copies ran while one was open for 61% of the time, Pallas kernels for 0%

profile of v1, /device:TPU:33, one launch (start us, length us, event | category | flops | bytes accessed | tf_op | source)
XLA Modules:
  0.0 232.0 jit_solution(1712068749454870083)
XLA Ops:
  0.6 1.6 copy.38
  2.8 1.5 pad_maximum_fusion
  4.3 4.7 %collective-permute-start.2 = (bf16[2,256,2048]{1,2,0:T(8,128)(2,1)}, bf16[2,256,2048]{1,2,0:T(8,128)(2,1)}, u32[]{:S(2)}, u32[]{:S(2)}) collective-permute-start(bf16[2,256,2048]{1,2,0:T(8,128)(2,1)} %pad_maximum_fusion), channel_id=1, source_target_pairs={{0,1},{1,2},{2,3},{3,4},{4,5},{5,6},{6,7},{7,8},{8,9},{9,10},{10,1... | collective-permute-start | bytes 6291464 | tf_op jit(solution)/shard_map/ppermute | solution.py:16
  9.0 4.6 %collective-permute-start.1 = (bf16[2,256,2048]{1,2,0:T(8,128)(2,1)}, bf16[2,256,2048]{1,2,0:T(8,128)(2,1)}, u32[]{:S(2)}, u32[]{:S(2)}) collective-permute-start(bf16[2,256,2048]{1,2,0:T(8,128)(2,1)} %pad_maximum_fusion), channel_id=1, source_target_pairs={{0,2},{1,3},{2,4},{3,5},{4,6},{5,7},{6,8},{7,9},{8,10},{9,11},{10,... | collective-permute-start | bytes 6291464 | tf_op jit(solution)/shard_map/ppermute | solution.py:16
  13.6 1.1 fusion.20
  14.7 3.3 %collective-permute-start = (bf16[2,128,2048]{1,2,0:T(8,128)(2,1)}, bf16[2,128,2048]{1,2,0:T(8,128)(2,1)}, u32[]{:S(2)}, u32[]{:S(2)}) collective-permute-start(bf16[2,128,2048]{1,2,0:T(8,128)(2,1)} %fusion.20), channel_id=1, source_target_pairs={{0,3},{1,4},{2,5},{3,6},{4,7},{5,8},{6,9},{7,10},{8,11},{9,12},{10... | collective-permute-start | bytes 3145736 | tf_op jit(solution)/shard_map/ppermute | solution.py:16
  96.2 28.1 %all-to-all-start = ((bf16[128,1,2,2,16,128]{5,4,3,2,1,0:T(8,128)(2,1)}), bf16[128,1,2,2,16,128]{5,4,3,2,1,0:T(8,128)(2,1)}, u32[]{:S(2)}, u32[]{:S(2)}) async-start(bf16[128,1,2,2,16,128]{5,4,3,2,1,0:T(8,128)(2,1)} %constant_dynamic-update-slice_fusion), calls=%async_computation | async-start | bytes 4194304 | tf_op jit(solution)/shard_map/all_to_all | solution.py:61
  126.0 2.3 copy.36
  128.5 3.5 %maximum_maximum_fusion = bf16[2,896,2048]{1,2,0:T(8,128)(2,1)S(1)} fusion(bf16[1,256,2048]{1,2,0:T(8,128)(2,1)S(1)} %bitcast.589, bf16[1,256,2048]{1,2,0:T(8,128)(2,1)S(1)} %bitcast.592, bf16[2,256,2048]{1,2,0:T(8,128)(2,1)} %collective-permute-done.2, bf16[2,256,2048]{1,2,0:T(8,128)(2,1)} %collective-permute-done.1, ...), kind=kLoop, calls=%fused_computation.22 | loop fusion | flops 36700160 | bytes 14680064 | tf_op jit(solution)/shard_map/concatenate | solution.py:76
  132.0 3.6 %fusion.26 = (bf16[1,896,2048]{1,2,0:T(8,128)(2,1)}, bf16[1,896,2048]{1,2,0:T(8,128)(2,1)}) fusion(bf16[2,896,2048]{1,2,0:T(8,128)(2,1)S(1)} %maximum_maximum_fusion), kind=kLoop, calls=%fused_computation.327 | loop fusion | bytes 14680064 | tf_op jit(solution)/shard_map/slice | solution.py:101
  135.6 51.0 %while.11 = (s32[]{:T(128)}, bf16[16,256,128]{2,1,0:T(8,128)(2,1)S(1)}, bf16[16,256,128]{1,2,0:T(8,128)(2,1)}, bf16[16,896,128]{1,2,0:T(8,128)(2,1)}, bf16[16,89...) while((s32[]{:T(128)}, ...), condition=%wide.region_9.10_spmd.clone, body=%wide.region_6.0_spmd.clone.sunk | while | flops 119995904 | bytes 3424237 | solution.py:118
  135.6 1.5 fusion.35
  137.4 1.3 fusion.37
  138.8 1.5 fusion.35
  140.6 1.3 fusion.37
  142.0 1.5 fusion.35
  143.8 1.3 fusion.37
  145.1 1.5 fusion.35
  147.0 1.3 fusion.37
  148.3 1.5 fusion.35
  150.2 1.3 fusion.37
  151.5 1.5 fusion.35
  153.4 1.3 fusion.37
  154.7 1.5 fusion.35
  156.6 1.3 fusion.37
  157.9 1.5 fusion.35
  159.8 1.3 fusion.37
  161.1 1.5 fusion.35
  162.9 1.3 fusion.37
  164.3 1.5 fusion.35
  166.1 1.3 fusion.37
  167.5 1.5 fusion.35
  169.3 1.3 fusion.37
  170.7 1.5 fusion.35
  172.5 1.3 fusion.37
  173.9 1.5 fusion.35
  175.7 1.3 fusion.37
  177.1 1.5 fusion.35
  178.9 1.3 fusion.37
  180.3 1.5 fusion.35
  182.1 1.3 fusion.37
  183.4 1.5 fusion.35
  185.3 1.3 fusion.37
  186.6 1.2 fusion.19
  187.9 35.5 %all-to-all-done = bf16[128,1,2,2,16,128]{5,4,3,2,1,0:T(8,128)(2,1)} async-done(((bf16[128,1,2,2,16,128]{5,4,3,2,1,0:T(8,128)(2,1)}), bf16[128,1,2,2,16,128]{5,4,3,2,1,0:T(8,128)(2,1)}, u32[]{:S(2)}, u32[]{:S(2)}) %all-to-all-start) | async-done | bytes 2097184 | tf_op jit(solution)/shard_map/all_to_all | solution.py:61
  223.4 3.3 %copy.44 = bf16[1,2,128,2,16,128]{5,4,3,2,1,0:T(8,128)(2,1)} copy(bf16[1,2,128,2,16,128]{5,4,3,1,0,2:T(8,128)(2,1)} %bitcast.144) | data formatting | bytes 4194304 | tf_op jit(solution)/shard_map/reshape | solution.py:60
  226.7 2.7 %gather_fusion = bf16[256,2,16,128]{3,2,1,0:T(8,128)(2,1)S(1)} fusion(bf16[2,256,16,128]{3,2,1,0:T(8,128)(2,1)} %bitcast.721, s32[1024]{0:T(1024)S(1)} %pad_clamp_fusion), kind=kCustom, calls=%fused_computation | custom fusion | bytes 4195328 | tf_op jit(solution)/shard_map/jit(_take)/gather | solution.py:63
  230.3 1.7 slice_bitcast_fusion
  (191 shorter events, 86.4 us)
Async XLA Ops:
  0.6 1.6 copy-start.1
  4.3 13.7 %copy-start = (bf16[256,2048]{1,0:T(8,128)(2,1)S(1)}, bf16[256,2048]{1,0:T(8,128)(2,1)}, u32[]{:S(2)}) copy-start(bf16[256,2048]{1,0:T(8,128)(2,1)} %param.11) | copy-start | bytes 3145732
  4.3 124.2 %collective-permute-start.2 = (bf16[2,256,2048]{1,2,0:T(8,128)(2,1)}, bf16[2,256,2048]{1,2,0:T(8,128)(2,1)}, u32[]{:S(2)}, u32[]{:S(2)}) collective-permute-start(bf16[2,256,2048]{1,2,0:T(8,128)(2,1)} %pad_maximum_fusion), channel_id=1, source_target_pairs={{0,1},{1,2},{2,3},{3,4},{4,5},{5,6},{6,7},{7,8},{8,9},{9,10},{10,1... | collective-permute-start | bytes 6291464 | tf_op jit(solution)/shard_map/ppermute | solution.py:16
  9.0 119.5 %collective-permute-start.1 = (bf16[2,256,2048]{1,2,0:T(8,128)(2,1)}, bf16[2,256,2048]{1,2,0:T(8,128)(2,1)}, u32[]{:S(2)}, u32[]{:S(2)}) collective-permute-start(bf16[2,256,2048]{1,2,0:T(8,128)(2,1)} %pad_maximum_fusion), channel_id=1, source_target_pairs={{0,2},{1,3},{2,4},{3,5},{4,6},{5,7},{6,8},{7,9},{8,10},{9,11},{10,... | collective-permute-start | bytes 6291464 | tf_op jit(solution)/shard_map/ppermute | solution.py:16
  14.7 113.8 %collective-permute-start = (bf16[2,128,2048]{1,2,0:T(8,128)(2,1)}, bf16[2,128,2048]{1,2,0:T(8,128)(2,1)}, u32[]{:S(2)}, u32[]{:S(2)}) collective-permute-start(bf16[2,128,2048]{1,2,0:T(8,128)(2,1)} %fusion.20), channel_id=1, source_target_pairs={{0,3},{1,4},{2,5},{3,6},{4,7},{5,8},{6,9},{7,10},{8,11},{9,12},{10... | collective-permute-start | bytes 3145736 | tf_op jit(solution)/shard_map/ppermute | solution.py:16
  96.1 28.1 %copy-start.5 = (s32[64]{0:T(128)S(1)}, s32[64]{0:T(128)}, u32[]{:S(2)}) copy-start(s32[64]{0:T(128)} %param.12) | copy-start | bytes 772
  96.1 28.2 %copy-start.2 = (s32[128]{0:T(128)S(1)}, s32[128]{0:T(128)}, u32[]{:S(2)}) copy-start(s32[128]{0:T(128)} %param.14) | copy-start | bytes 1540
  96.1 28.2 %copy-start.4 = (s32[128]{0:T(128)S(1)}, s32[128]{0:T(128)}, u32[]{:S(2)}) copy-start(s32[128]{0:T(128)} %param.13) | copy-start | bytes 1540
  96.1 29.1 %copy-start.3 = (s32[64]{0:T(128)S(1)}, s32[64]{0:T(128)}, u32[]{:S(2)}) copy-start(s32[64]{0:T(128)} %param.15) | copy-start | bytes 772
  96.2 127.2 %all-to-all-start = ((bf16[128,1,2,2,16,128]{5,4,3,2,1,0:T(8,128)(2,1)}), bf16[128,1,2,2,16,128]{5,4,3,2,1,0:T(8,128)(2,1)}, u32[]{:S(2)}, u32[]{:S(2)}) async-start(bf16[128,1,2,2,16,128]{5,4,3,2,1,0:T(8,128)(2,1)} %constant_dynamic-update-slice_fusion), calls=%async_computation | async-start | bytes 4194304 | tf_op jit(solution)/shard_map/all_to_all | solution.py:61
